TPU v7x, 32 devices: a whole 2x2x4 slice. The times are simulated.
32 devices in a mesh: ep: 4 (over z), dp: 8 (over y, x, core).
Axes of the slice: x: 2, y: 2, z: 4, core: 2. Of those that a mesh axis runs over, the one named last changes fastest.
Arguments:
- tokens: bfloat16 [16384, 256], P(('dp', 'ep'))
- dy_out: bfloat16 [16384, 256], P(('dp', 'ep'))
- dense_w1: bfloat16 [256, 256], replicated
- route_idx1: int32 [16384, 2], P(('dp', 'ep'))
- route_gate1: float32 [16384, 2], P(('dp', 'ep'))
- w_gate1: bfloat16 [8, 256, 896], P('ep')
- w_up1: bfloat16 [8, 256, 896], P('ep')
- w_down1: bfloat16 [8, 896, 256], P('ep')
- dense_w2: bfloat16 [256, 256], replicated
- route_idx2: int32 [16384, 2], P(('dp', 'ep'))
- route_gate2: float32 [16384, 2], P(('dp', 'ep'))
- w_gate2: bfloat16 [8, 256, 896], P('ep')
- w_up2: bfloat16 [8, 256, 896], P('ep')
- w_down2: bfloat16 [8, 896, 256], P('ep')
Outputs:
- output 1: bfloat16 [16384, 256], P(('dp', 'ep'))
- output 2: bfloat16 [256, 256], P(('dp', 'ep'))
- output 3: bfloat16 [8, 256, 896], P('ep', 'dp')
- output 4: bfloat16 [8, 256, 896], P('ep', 'dp')
- output 5: bfloat16 [8, 896, 256], P('ep', None, 'dp')
- output 6: bfloat16 [256, 256], P(('dp', 'ep'))
- output 7: bfloat16 [8, 256, 896], P('ep', 'dp')
- output 8: bfloat16 [8, 256, 896], P('ep', 'dp')
- output 9: bfloat16 [8, 896, 256], P('ep', None, 'dp')
All inputs are finite; a program needn't handle non-finite values.
Results may differ from a plain program's by a relative error of at most 0.02.
Values are sent between devices in bfloat16 or wider.
A program may use at most 1 GiB of HBM per device.

v0:
```python
import functools

import jax
import jax.numpy as jnp
from jax import lax
from jax.experimental import pallas as pl
from jax.experimental.pallas import tpu as pltpu
from jax.sharding import PartitionSpec as P

MESH = pl.DeviceIdType.MESH
F32, BF16 = jnp.float32, jnp.bfloat16
N_EP = 4
N_EXP = 8
CAP = 256


def nn(a, b):
    return lax.dot_general(a, b, (((1,), (0,)), ((), ())), preferred_element_type=F32)


def nt(a, b):
    return lax.dot_general(a, b, (((1,), (1,)), ((), ())), preferred_element_type=F32)


def tn(a, b):
    return lax.dot_general(a, b, (((0,), (0,)), ((), ())), preferred_element_type=F32)


def kernel(n_dp, x_ref, dy_ref, dense1, dense2, idx1, gate1, idx2, gate2,
           wg1_hbm, wu1_hbm, wd1_hbm, wg2_hbm, wu2_hbm, wd2_hbm,
           tok_out, exp_out,
           w_gate, w_up, w_down, auxs, auxb, posr, gater, posc, gatec, tri, ag, ret, x_end, merge_in, rows_in, t_a, t_b, t_gh, hid, g_a, g_b, g_out,
           acc, g_mix, part, gs, gr, g2, g3, d_send, d_a, d_bs, d_b, exp_v, dx_v, den_v,
           w_sem, aux_send, aux_recv, ag_right, ag_left, ag_recv, ret_send, ret_recv, end_send, end_recv, pair_send, pair_recv,
           one_send, one_recv, two_send, two_recv, da_send, da_recv, db_send, db_recv, out_sem):
    z = lax.axis_index('ep')
    dp = lax.axis_index('dp')
    n_chip = n_dp // 2
    core = dp % 2
    chip = dp // 2
    n_tok, d_model = x_ref.shape
    d_ff = t_a.shape[2]
    piece = d_model // n_dp

    def swapped(k):
        return jnp.where(k < 2, 1 - k, k)

    def order(k):
        low = jnp.where(jnp.logical_or(z == 1, z == 2), swapped(k), k)
        return jnp.where(z < 2, low, 3 - low)

    def order_owned(k):
        low = swapped(k)
        return jnp.where(z < 2, low, 3 - low)

    def owner(s):
        return jnp.where(s < 2, 1, 2)

    inner = jnp.logical_or(z == 1, z == 2)
    outer = jnp.logical_not(inner)
    near_mid = jnp.where(z < 2, 1, 2)
    near_end = jnp.where(z < 2, 0, 3)

    barrier = pltpu.get_barrier_semaphore()
    for k in range(1, N_EP):
        pl.semaphore_signal(barrier, inc=1, device_id={'ep': (z + k) % N_EP, 'dp': dp}, device_id_type=MESH)
    for k in range(1, n_dp):
        pl.semaphore_signal(barrier, inc=1, device_id={'ep': z, 'dp': (dp + k) % n_dp}, device_id_type=MESH)

    w_copies = []
    for n, (hbm, dst) in enumerate(((wg1_hbm, w_gate.at[0]), (wu1_hbm, w_up.at[0]), (wd1_hbm, w_down.at[0]),
                                    (wg2_hbm, w_gate.at[1]), (wu2_hbm, w_up.at[1]), (wd2_hbm, w_down.at[1]))):
        w_copies.append(pltpu.make_async_copy(hbm, dst, w_sem.at[n]))
        w_copies[-1].start()

    auxs[0:2] = idx1[...].astype(F32)
    auxs[2:4] = gate1[...]
    auxs[4:6] = idx2[...].astype(F32)
    auxs[6:8] = gate2[...]
    x = x_ref[...]
    ag[0, z] = (x.astype(F32) + nn(x, dense1[...])).astype(BF16)
    ag[2, z] = dy_ref[...]
    auxb[z] = auxs[...]

    pl.semaphore_wait(barrier, N_EP - 1 + n_dp - 1)

    def col_copy(src, dst, send, recv, to):
        return pltpu.make_async_remote_copy(src_ref=src, dst_ref=dst, send_sem=send, recv_sem=recv,
                                            device_id={'ep': to, 'dp': dp}, device_id_type=MESH)

    def row_copy(src, dst, send, recv, to):
        return pltpu.make_async_remote_copy(src_ref=src, dst_ref=dst, send_sem=send, recv_sem=recv,
                                            device_id={'ep': z, 'dp': to}, device_id_type=MESH)

    def aux_copy(k):
        return col_copy(auxs, auxb.at[z], aux_send.at[k], aux_recv.at[z], (z + k) % N_EP)

    for k in range(1, N_EP):
        aux_copy(k).start()

    def ag_to_right(n, s):
        return col_copy(ag.at[n, s], ag.at[n, s], ag_right.at[n, s], ag_recv.at[n, s], jnp.minimum(z + 1, N_EP - 1))

    def ag_to_left(n, s):
        return col_copy(ag.at[n, s], ag.at[n, s], ag_left.at[n, s], ag_recv.at[n, s], jnp.maximum(z - 1, 0))

    def rightward(n, s):
        return jnp.logical_and((owner(s) if n % 2 else s) <= z, z < N_EP - 1)

    def leftward(n, s):
        return jnp.logical_and((owner(s) if n % 2 else s) >= z, z > 0)

    def ag_pass(n, s, right=True, left=True):
        if right is not False:
            @pl.when(jnp.logical_and(rightward(n, s), right))
            def _():
                ag_to_right(n, s).start()

        if left is not False:
            @pl.when(jnp.logical_and(leftward(n, s), left))
            def _():
                ag_to_left(n, s).start()

    def ag_take(n, s):
        ag_to_right(n, s).wait_recv()
        ag_pass(n, s)

    def ag_step(n, k):
        @pl.when(k == 1)
        def _():
            ag_take(n, order(1))

        @pl.when(jnp.logical_or(jnp.logical_and(k == 1, inner), jnp.logical_and(k == 2, outer)))
        def _():
            ag_take(n, order(2))

        @pl.when(k == 3)
        def _():
            ag_take(n, order(3))

    def owned_step(n, k, s, early):
        if early:
            @pl.when(jnp.logical_and(k == 0, inner))
            def _():
                ag_take(n, order_owned(2))

            @pl.when(jnp.logical_and(k == 2, inner))
            def _():
                ag_take(n, order_owned(3))

        @pl.when(outer if early else jnp.logical_or(k > 1, outer))
        def _():
            ag_take(n, s)

    def ag_drain(n):
        def body(s, carry):
            @pl.when(rightward(n, s))
            def _():
                ag_to_right(n, s).wait_send()

            @pl.when(leftward(n, s))
            def _():
                ag_to_left(n, s).wait_send()
            return carry
        lax.fori_loop(0, N_EP, body, 0)

    def ret_at(s):
        return jnp.where(owner(s) == z, N_EP + s % 2 * N_EP + z, s)

    def ret_copy(n, s):
        return col_copy(ret.at[n, s], ret.at[n, N_EP + s % 2 * N_EP + z], ret_send.at[n, s], ret_recv.at[n, s % 2 * N_EP + z], owner(s))

    def ret_start(n, s):
        @pl.when(owner(s) != z)
        def _():
            ret_copy(n, s).start()

    def ret_wait(n, p, frm):
        at = p * N_EP + frm
        col_copy(ret.at[n, 0], ret.at[n, N_EP + at], ret_send.at[n, 0], ret_recv.at[n, at], z).wait_recv()

    def ret_drain(n):
        def body(s, carry):
            away = owner(s) != z

            @pl.when(jnp.logical_and(away, jnp.logical_or(inner, s != order_owned(2))) if n == 2 else away)
            def _():
                ret_copy(n, s).wait_send()
            return carry
        lax.fori_loop(0, N_EP, body, 0)

    def merge_copy():
        return col_copy(ret.at[2, order_owned(2)], merge_in, end_send.at[2], end_recv.at[2], near_mid)

    def x_copy():
        return col_copy(x_ref, x_end, end_send.at[0], end_recv.at[0], near_mid)

    def dx_back():
        return col_copy(g_mix.at[0], dx_v, end_send.at[1], end_recv.at[1], near_end)

    ag_pass(0, z)
    ag_pass(2, z, right=z == 1, left=z == 2)

    r_io = lax.broadcasted_iota(jnp.int32, (n_tok, n_tok), 0)
    c_io = lax.broadcasted_iota(jnp.int32, (n_tok, n_tok), 1)
    tri[...] = (c_io < r_io).astype(F32).astype(BF16)
    lane = lax.broadcasted_iota(jnp.int32, (n_tok, N_EXP), 1)
    for k in range(1, N_EP):
        s = (z + k) % N_EP
        col_copy(auxs, auxb.at[s], aux_send.at[k], aux_recv.at[s], s).wait_recv()
    for p in range(2):
        cols = auxb[jnp.where(z < 2, 0, 2) + p].T
        hit0 = cols[:, 0:1] == lane.astype(F32)
        hit1 = cols[:, 1:2] == lane.astype(F32)
        hit = jnp.logical_or(hit0, hit1)
        rank = nn(tri[...], hit.astype(F32).astype(BF16))
        posc[p] = jnp.where(hit, rank, -1.0)
        gatec[p] = jnp.where(hit0, cols[:, 2:3], 0.0) + jnp.where(hit1, cols[:, 3:4], 0.0)
    hits = []
    for layer in range(2):
        for s in range(N_EP):
            for e in range(2):
                a = auxb[s]
                expert = (z * 2 + e).astype(F32)
                hit0 = a[4 * layer:4 * layer + 1] == expert
                hit1 = a[4 * layer + 1:4 * layer + 2] == expert
                hits.append(jnp.logical_or(hit0, hit1).astype(F32))
                gater[(layer * N_EP + s) * 2 + e] = (jnp.where(hit0, a[4 * layer + 2:4 * layer + 3], 0.0)
                                                     + jnp.where(hit1, a[4 * layer + 3:4 * layer + 4], 0.0))
    stack = jnp.concatenate(hits, axis=0)
    ranks = jnp.where(stack > 0.5, nt(stack.astype(BF16), tri[...]), -1.0)
    for n in range(4 * N_EP):
        posr[n] = ranks[n:n + 1]

    for copy in w_copies:
        copy.wait()

    slot = lax.broadcasted_iota(jnp.int32, (CAP, n_tok), 0).astype(F32)
    slot_lane = lax.broadcasted_iota(jnp.int32, (n_tok, CAP), 1).astype(F32)
    step = 32

    def select(layer, s):
        at = (layer * N_EP + s) * 2
        return [posr[at + e] == slot for e in range(2)]

    def as_bf16(picks):
        return jnp.concatenate([p.astype(F32).astype(BF16) for p in picks], axis=0)

    def take_rows(layer, s, n, pick):
        u = ag[n, s]
        if n == 1:
            u = (u.astype(F32) + nn(u, dense2[...])).astype(BF16)
        rows = nn(pick, u).astype(BF16)
        for e in range(2):
            rows_in[layer, e, s] = rows[e * CAP:(e + 1) * CAP]

    def up_project(layer, s, e):
        rows = rows_in[layer, e, s]
        t_a[e] = nn(rows, w_gate[layer, e])
        t_b[e] = nn(rows, w_up[layer, e])

    def forward(s):
        take_rows(0, s, 0, as_bf16(select(0, s)))
        for e in range(2):
            up_project(0, s, e)
        for e in range(2):
            for i in range(CAP // step):
                r = pl.ds(i * step, step)
                a = t_a[e, r, :]
                hid[e, s, r, :] = (a * jax.nn.sigmoid(a) * t_b[e, r, :]).astype(BF16)
            ret[0, ret_at(s), e * CAP:(e + 1) * CAP] = nn(hid[e, s], w_down[0, e]).astype(BF16)

    def backward(layer, s, n_dy, n_ret, n_u):
        picks = select(layer, s)
        pick = as_bf16(picks)
        at = (layer * N_EP + s) * 2
        if n_u is not None:
            take_rows(layer, s, n_u, pick)
        got = nn(pick, ag[n_dy, s])
        for e in range(2):
            gate = jnp.sum(jnp.where(picks[e], gater[at + e], 0.0), axis=1, keepdims=True)
            g_out[e, s] = (got[e * CAP:(e + 1) * CAP] * gate).astype(BF16)
        for e in range(2):
            up_project(layer, s, e)
            t_gh[e] = nt(g_out[e, s], w_down[layer, e]).astype(BF16)
        parts = []
        for e in range(2):
            for i in range(CAP // step):
                r = pl.ds(i * step, step)
                a = t_a[e, r, :]
                b = t_b[e, r, :]
                gh = t_gh[e, r, :].astype(F32)
                sig = jax.nn.sigmoid(a)
                act = a * sig
                hid[e, s, r, :] = (act * b).astype(BF16)
                g_a[e, s, r, :] = (gh * b * sig * (1.0 + a * (1.0 - sig))).astype(BF16)
                g_b[e, s, r, :] = (gh * act).astype(BF16)
            parts.append((nt(g_a[e, s], w_gate[layer, e]) + nt(g_b[e, s], w_up[layer, e])).astype(BF16))
        ret[n_ret, ret_at(s)] = tn(pick, jnp.concatenate(parts, axis=0)).astype(BF16)

    def mix(p, base):
        acc[...] = base.astype(F32)

        def body(k, carry):
            s = order(k)

            @pl.when(k > 0)
            def _():
                ret_wait(0, p, s)

            for e in range(2):
                here = lane == s * 2 + e
                pos = jnp.sum(jnp.where(here, posc[p], 0.0), axis=1, keepdims=True)
                weight = jnp.sum(jnp.where(here, gatec[p], 0.0), axis=1, keepdims=True)
                hot = (pos == slot_lane).astype(F32).astype(BF16)
                acc[...] += nn(hot, ret[0, N_EP + p * N_EP + s, e * CAP:(e + 1) * CAP]) * weight
            return carry
        lax.fori_loop(0, N_EP, body, 0)
        return acc[...].astype(BF16)

    def add_up(n, p, base, n_from=N_EP):
        total = base.astype(F32) + ret[n, N_EP + p * N_EP + z].astype(F32)
        for k in range(1, n_from):
            ret_wait(n, p, order(k))
            total += ret[n, N_EP + p * N_EP + order(k)].astype(F32)
        return total.astype(BF16)

    chip_x = chip % 2
    chip_y = chip // 2
    over_x = chip + 1 - 2 * chip_x
    over_y = (chip + 2) % n_chip

    def group(e):
        return jnp.where(e == 0, chip_x, chip_y)

    def place(e):
        return jnp.where(e == 0, chip_y, chip_x)

    def pair_copy(layer, e, q):
        return row_copy(gs.at[1 - core, e, q], gr.at[layer, e, q], pair_send.at[layer, e, q], pair_recv.at[layer, e, q], chip * 2 + 1 - core)

    def one_copy(layer, e, q):
        return row_copy(gr.at[layer, e, q, 1 - group(e)], g2.at[layer, e, q], one_send.at[layer, e, q], one_recv.at[layer, e, q],
                        jnp.where(e == 0, over_x, over_y) * 2 + core)

    def two_copy(layer, e, q):
        return row_copy(gr.at[layer, e, q, group(e), 1 - place(e)], g3.at[layer, e, q], two_send.at[layer, e, q], two_recv.at[layer, e, q],
                        jnp.where(e == 0, over_y, over_x) * 2 + core)

    def pair_finish(layer, e, q):
        pair_copy(layer, e, q).wait()
        for g in range(2):
            for p in range(2):
                gr[layer, e, q, g, p] = (gr[layer, e, q, g, p].astype(F32) + gs[core, e, q, g, p].astype(F32)).astype(BF16)
        one_copy(layer, e, q).start()

    def one_finish(layer):
        def body(n, carry):
            e, q = n % 2, (n // 2 + 2) % 3
            one_copy(layer, e, q).wait_recv()
            for p in range(2):
                gr[layer, e, q, group(e), p] = (gr[layer, e, q, group(e), p].astype(F32) + g2[layer, e, q, p].astype(F32)).astype(BF16)
            two_copy(layer, e, q).start()
            return carry
        lax.fori_loop(0, 6, body, 0)

    def two_finish(layer):
        def body(n, carry):
            e, q = n % 2, (n // 2 + 2) % 3
            two_copy(layer, e, q).wait_recv()
            exp_v[layer, q * 2 + e] = (gr[layer, e, q, group(e), place(e)].astype(F32) + g3[layer, e, q].astype(F32)).astype(BF16)
            one_copy(layer, e, q).wait_send()
            two_copy(layer, e, q).wait_send()
            return carry
        lax.fori_loop(0, 6, body, 0)
        exp_copy(layer).start()

    def exp_copy(layer):
        return pltpu.make_async_copy(exp_v.at[layer], exp_out.at[layer], out_sem.at[layer])

    def operands(layer, e, at, n):
        rows = rows_in[layer, e, pl.ds(at, n)].reshape(n * CAP, d_model)
        outs = g_out[e, pl.ds(at, n)].reshape(n * CAP, d_model)
        return [(j, left, right[e, pl.ds(at, n)].reshape(n * CAP, d_ff))
                for j, left, right in ((2, outs, hid), (0, rows, g_a), (1, rows, g_b))]

    def weight_part(layer, at, n):
        def body(e, carry):
            for j, left, right in operands(layer, e, at, n):
                part[e, j] = tn(left, right)
            return carry
        lax.fori_loop(0, 2, body, 0)

    def split_grad(layer, e, j, grad):
        for p in range(n_dp):
            y, x = p // 4, p // 2 % 2
            gs[p % 2, e, j, jnp.where(e == 0, x, y), jnp.where(e == 0, y, x)] = grad[p * piece:(p + 1) * piece].astype(BF16)
        pair_copy(layer, e, j).start()

    def weight_grads(layer):
        def body(e, carry):
            for j, left, right in operands(layer, e, 0, N_EP):
                split_grad(layer, e, j, tn(left, right))
            return carry
        lax.fori_loop(0, 2, body, 0)
        for j in (2, 0, 1):
            for e in range(2):
                pair_finish(layer, e, j)

    def weight_rest(layer, at):
        both = [operands(layer, e, at, 2) for e in range(2)]
        todo = [(e, both[e][q]) for q in range(3) for e in range(2)]
        for k, (e, (j, left, right)) in enumerate(todo):
            split_grad(layer, e, j, tn(left, right) + part[e, j])
            if k >= 2:
                pair_finish(layer, todo[k - 2][0], todo[k - 2][1][0])
        for e, (j, _, _) in todo[4:]:
            pair_finish(layer, e, j)

    sub = piece // N_EP

    def da_copy(layer, k):
        to = (z + k) % N_EP
        return col_copy(d_send.at[layer, to], d_a.at[layer, z], da_send.at[layer, k], da_recv.at[layer, z], to)

    def db_copy(layer, k):
        to = (dp + k) % n_dp
        return row_copy(d_bs.at[layer, to], d_b.at[layer, dp], db_send.at[layer, k], db_recv.at[layer, dp], to)

    def dense_start(layer, grad):
        for q in range(N_EP):
            for p in range(n_dp):
                at = p * piece + q * sub
                d_send[layer, q, p] = grad[at:at + sub].astype(BF16)
        for k in range(1, N_EP):
            da_copy(layer, k).start()
        d_a[layer, z] = d_send[layer, z]

    def dense_middle(layer):
        for m in (1, 2):
            @pl.when(z != m)
            def _():
                col_copy(d_send.at[layer, m], d_a.at[layer, m], da_send.at[layer, 0], da_recv.at[layer, m], m).wait_recv()
        d_bs[layer] = (d_a[layer, 1].astype(F32) + d_a[layer, 2].astype(F32)).astype(BF16)
        for k in range(1, n_dp):
            db_copy(layer, k).start()

    def dense_end(layer):
        total = d_bs[layer, dp].astype(F32)
        for k in range(1, n_dp):
            frm = (dp + k) % n_dp
            row_copy(d_bs.at[layer, frm], d_b.at[layer, frm], db_send.at[layer, k], db_recv.at[layer, frm], frm).wait_recv()
            total += d_b[layer, frm].astype(F32)
        den_v[layer * sub:(layer + 1) * sub] = total.astype(BF16)
        @pl.when(inner)
        def _():
            for k in range(1, N_EP):
                da_copy(layer, k).wait_send()
        for k in range(1, n_dp):
            db_copy(layer, k).wait_send()

    def forward_step(k, carry):
        s = order(k)
        ag_step(0, k)
        forward(s)
        ret_start(0, s)
        return carry
    lax.fori_loop(0, N_EP, forward_step, 0)

    ag_pass(2, z, right=z != 1, left=z != 2)

    @pl.when(outer)
    def _():
        x_copy().start()

    @pl.when(inner)
    def _():
        ag_take(2, 3 - z)

        def body(n, carry):
            s = jnp.where(n == 0, z, near_end)
            ag[1, s] = mix(s % 2, ag[0, s])
            ag_pass(1, s)

            @pl.when(n == 1)
            def _():
                ag_to_right(2, s).wait_recv()
                ag_pass(2, s, right=z == 1, left=z == 2)
            return carry
        lax.fori_loop(0, 2, body, 0)

    def second_step(k, carry):
        s = order_owned(k)

        owned_step(1, k, s, False)

        @pl.when(jnp.logical_or(k > 2, jnp.logical_and(outer, s != z)))
        def _():
            ag_take(2, s)
        backward(1, s, 2, 1, 1)
        ret_start(1, s)
        return carry
    lax.fori_loop(0, N_EP, second_step, 0)
    weight_grads(1)

    @pl.when(inner)
    def _():
        def body(n, carry):
            s = jnp.where(n == 0, z, near_end)
            gm = add_up(1, s % 2, ag[2, s])
            g_mix[n] = gm
            ag[3, s] = (gm.astype(F32) + nt(gm, dense2[...])).astype(BF16)
            ag_pass(3, s)
            return carry
        lax.fori_loop(0, 2, body, 0)
        dense_start(1, tn(ag[1, z], g_mix[0]) + tn(ag[1, near_end], g_mix[1]))

    early_at = jnp.where(z < 2, 0, 2)
    late_at = 2 - early_at

    def first_step(k, carry):
        s = order_owned(k)

        @pl.when(jnp.logical_and(k == 2, outer))
        def _():
            weight_part(0, early_at, 2)

        @pl.when(jnp.logical_and(k == 3, outer))
        def _():
            dense_middle(1)
            one_finish(1)
        owned_step(3, k, s, True)
        backward(0, s, 3, 2, None)

        @pl.when(k != 2)
        def _():
            ret_start(2, s)

        @pl.when(jnp.logical_and(k == 2, outer))
        def _():
            merge_copy().start()
        return carry
    lax.fori_loop(0, N_EP, first_step, 0)

    @pl.when(inner)
    def _():
        dense_middle(1)
        one_finish(1)
        weight_part(0, early_at, 2)
    weight_rest(0, late_at)
    for n in range(3):
        ag_drain(n)
    for n in range(2):
        ret_drain(n)

    @pl.when(outer)
    def _():
        x_copy().wait_send()
    for k in range(1, N_EP):
        aux_copy(k).wait_send()
    @pl.when(inner)
    def _():
        merge_copy().wait_recv()
        other = 3 - z
        ret[2, other] = (ret[2, other].astype(F32) + merge_in[...].astype(F32)).astype(BF16)
        ret_copy(2, other).start()
    one_finish(0)
    two_finish(1)
    dense_end(1)

    def dx_copy():
        return pltpu.make_async_copy(dx_v, tok_out.at[pl.ds(0, n_tok)], out_sem.at[2])

    @pl.when(inner)
    def _():
        gm = add_up(2, z % 2, ag[3, z], N_EP - 1)
        dx_v[...] = (gm.astype(F32) + nt(gm, dense1[...])).astype(BF16)
        dx_copy().start()
        ge = add_up(2, near_end % 2, ag[3, near_end])
        g_mix[0] = (ge.astype(F32) + nt(ge, dense1[...])).astype(BF16)
        x_copy().wait_recv()
        dense_start(0, tn(x_ref[...], gm) + tn(x_end[...], ge))
        dx_back().start()
    dense_middle(0)
    two_finish(0)

    @pl.when(outer)
    def _():
        dx_back().wait_recv()
        dx_copy().start()
        merge_copy().wait_send()
    dense_end(0)
    den_copy = pltpu.make_async_copy(den_v, tok_out.at[pl.ds(n_tok, 2 * sub)], out_sem.at[3])
    den_copy.start()
    ag_drain(3)
    ret_drain(2)

    @pl.when(inner)
    def _():
        dx_back().wait_send()
    exp_copy(1).wait()
    exp_copy(0).wait()
    dx_copy().wait()
    den_copy.wait()


def spread(n_tok, sub, tok, exp, *refs):
    outs, tok_v, exp_v, sem = refs[:9], refs[9], refs[10], refs[11]
    parts = [(tok, tok_v), (exp, exp_v)]
    for n, (src, dst) in enumerate(parts):
        pltpu.make_async_copy(src, dst, sem.at[n]).start()
    pltpu.make_async_copy(tok, tok_v, sem.at[0]).wait()
    copies = [(tok_v.at[pl.ds(0, n_tok)], outs[0])]
    for layer in range(2):
        copies.append((tok_v.at[pl.ds(n_tok + layer * sub, sub)], outs[1 + 4 * layer]))
    for layer in range(2):
        for q in range(3):
            copies.append((exp_v.at[layer, pl.ds(2 * q, 2)], outs[2 + 4 * layer + q]))
    for n, (src, dst) in enumerate(copies):
        if n == 3:
            pltpu.make_async_copy(exp, exp_v, sem.at[1]).wait()
        pltpu.make_async_copy(src, dst, sem.at[2 + n]).start()
    for n, (src, dst) in enumerate(copies):
        pltpu.make_async_copy(src, dst, sem.at[2 + n]).wait()


def solution(mesh):
    n_dp = mesh.shape['dp']
    n_chip = n_dp // 2
    tok_spec = P(('dp', 'ep'), None)
    exp_spec = P('ep', None, None)
    layer_specs = (P(None, None), tok_spec, tok_spec, exp_spec, exp_spec, exp_spec)
    grad_specs = (P(('dp', 'ep'), None), P('ep', 'dp', None), P('ep', 'dp', None), P('ep', None, 'dp'))

    def local_step(tokens, dy_out, dense_w1, idx1, gate1, wg1, wu1, wd1, dense_w2, idx2, gate2, wg2, wu2, wd2):
        n_tok, d_model = tokens.shape
        d_ff = wg1.shape[2]
        piece = d_model // n_dp
        sub = piece // N_EP
        vmem = pl.BlockSpec(memory_space=pltpu.VMEM)
        hbm = pl.BlockSpec(memory_space=pl.ANY)
        dma = pltpu.SemaphoreType.DMA
        six = (2, 2, 3)
        outs = pl.pallas_call(
            functools.partial(kernel, n_dp),
            out_shape=(jax.ShapeDtypeStruct((n_tok + 2 * sub, d_model), BF16), jax.ShapeDtypeStruct((2, 6, piece, d_ff), BF16)),
            in_specs=[vmem] * 8 + [hbm] * 6,
            out_specs=[hbm] * 2,
            scratch_shapes=[
                pltpu.VMEM((2, 2, d_model, d_ff), BF16), pltpu.VMEM((2, 2, d_model, d_ff), BF16), pltpu.VMEM((2, 2, d_ff, d_model), BF16),
                pltpu.VMEM((8, n_tok), F32), pltpu.VMEM((N_EP, 8, n_tok), F32), pltpu.VMEM((4 * N_EP, 1, n_tok), F32), pltpu.VMEM((4 * N_EP, 1, n_tok), F32),
                pltpu.VMEM((2, n_tok, N_EXP), F32), pltpu.VMEM((2, n_tok, N_EXP), F32), pltpu.VMEM((n_tok, n_tok), BF16),
                pltpu.VMEM((4, N_EP, n_tok, d_model), BF16), pltpu.VMEM((3, 3 * N_EP, n_tok, d_model), BF16),
                pltpu.VMEM((n_tok, d_model), BF16), pltpu.VMEM((n_tok, d_model), BF16),
                pltpu.VMEM((2, 2, N_EP, CAP, d_model), BF16), pltpu.VMEM((2, CAP, d_ff), F32), pltpu.VMEM((2, CAP, d_ff), F32),
                pltpu.VMEM((2, CAP, d_ff), BF16), pltpu.VMEM((2, N_EP, CAP, d_ff), BF16), pltpu.VMEM((2, N_EP, CAP, d_ff), BF16),
                pltpu.VMEM((2, N_EP, CAP, d_ff), BF16), pltpu.VMEM((2, N_EP, CAP, d_model), BF16),
                pltpu.VMEM((n_tok, d_model), F32), pltpu.VMEM((2, n_tok, d_model), BF16),
                pltpu.VMEM((2, 3, d_model, d_ff), F32),
                *[pltpu.VMEM(six + (2, 2, piece, d_ff), BF16)] * 2, pltpu.VMEM(six + (2, piece, d_ff), BF16), pltpu.VMEM(six + (piece, d_ff), BF16),
                pltpu.VMEM((2, N_EP, n_dp, sub, d_model), BF16), pltpu.VMEM((2, N_EP, n_dp, sub, d_model), BF16),
                pltpu.VMEM((2, n_dp, sub, d_model), BF16), pltpu.VMEM((2, n_dp, sub, d_model), BF16),
                pltpu.VMEM((2, 6, piece, d_ff), BF16), pltpu.VMEM((n_tok, d_model), BF16), pltpu.VMEM((2 * sub, d_model), BF16),
                dma((6,)), dma((N_EP,)), dma((N_EP,)), *[dma((4, N_EP))] * 3, dma((3, N_EP)), dma((3, 2 * N_EP)),
                dma((3,)), dma((3,)), *[dma(six)] * 6, *[dma((2, N_EP))] * 2, *[dma((2, n_dp))] * 2, dma((4,)),
            ],
            compiler_params=pltpu.CompilerParams(collective_id=0, has_side_effects=True, vmem_limit_bytes=67043328),
        )(tokens, dy_out, dense_w1, dense_w2, idx1.T, gate1.T, idx2.T, gate2.T, wg1, wu1, wd1, wg2, wu2, wd2)
        tok, exp = outs
        grads = [jax.ShapeDtypeStruct((sub, d_model), BF16)] + [jax.ShapeDtypeStruct((2, piece, d_ff), BF16)] * 3
        res = list(pl.pallas_call(
            functools.partial(spread, n_tok, sub),
            out_shape=tuple([jax.ShapeDtypeStruct((n_tok, d_model), BF16)] + grads * 2),
            in_specs=[hbm] * 2,
            out_specs=[hbm] * 9,
            scratch_shapes=[pltpu.VMEM((n_tok + 2 * sub, d_model), BF16), pltpu.VMEM((2, 6, piece, d_ff), BF16), dma((11,))],
        )(tok, exp))
        for n in (4, 8):
            res[n] = jnp.swapaxes(res[n], 1, 2)
        return tuple(res)

    return jax.shard_map(local_step, mesh=mesh, in_specs=(tok_spec, tok_spec) + layer_specs + layer_specs,
                         out_specs=(tok_spec,) + grad_specs + grad_specs, check_vma=False)
```

profile of v0, /device:TPU:0, one launch (start us, length us, event | category | flops | bytes accessed | tf_op | source)
XLA Modules:
  0.0 138.8 jit_solution(16896985265627840032)
XLA Ops:
  0.6 135.9 %shard_map.205 = (bf16[528,256]{1,0:T(8,128)(2,1)}, bf16[2,6,32,896]{3,2,1,0:T(8,128)(2,1)}) custom-call(bf16[512,256]{1,0:T(8,128)(2,1)} %x_ref.1, bf16[512,256]{1,0:T(8,128)(2,1)} %dy_ref.1, bf16[256,256]{1,0:T(8,128)(2,1)} %dense1.1, bf16[256,256]{1,0:T(8,128)(2,1)} %dense2.1, s32[2,512]{1,0:T(2,128)} %bitcast.6, f32[2,512]{1,0:T(2,128)} %bitcast.7, ...), custom_call_target="tpu_custom_call" | custom-call | tf_op jit(solution)/shard_map/pallas_call | solution.py:644
  136.5 2.1 %shard_map.206 = (bf16[512,256]{1,0:T(8,128)(2,1)}, bf16[8,256]{1,0:T(8,128)(2,1)}, bf16[2,32,896]{2,1,0:T(8,128)(2,1)}, bf16[2,32,896]{2,1,0:T(8,128)(2,1)}, bf...) custom-call(bf16[528,256]{1,0:T(8,128)(2,1)} %get-tuple-element.20.t, ...), custom_call_target="tpu_custom_call" | custom-call | tf_op jit(solution)/shard_map/pallas_call | solution.py:671
where the time goes:
time: 139 us
  Pallas kernels  138 us (99%)
    pallas_call x1, Pallas kernels, local_step(): pl.pallas_call(functools.partial(kernel, n_dp), out_shape=(jax.ShapeDtype...  136 us

commit v1 on v0

--- a/solution.py
+++ b/solution.py
@@ -140,11 +140,11 @@
 
     def owned_step(n, k, s, early):
         if early:
-            @pl.when(jnp.logical_and(k == 0, inner))
+            @pl.when(jnp.logical_and(k == 1, inner))
             def _():
                 ag_take(n, order_owned(2))
 
-            @pl.when(jnp.logical_and(k == 2, inner))
+            @pl.when(jnp.logical_and(k == 3, inner))
             def _():
                 ag_take(n, order_owned(3))
 

time: 139 us -> 138 us (level)
  no operation moved by 1% of the time
where the time goes in v1:
time: 138 us
  Pallas kernels  138 us (100%)
    pallas_call x1, Pallas kernels, local_step(): pl.pallas_call(functools.partial(kernel, n_dp), out_shape=(jax.ShapeDtype...  135 us

profile of v1, /device:TPU:0, one launch (start us, length us, event | category | flops | bytes accessed | tf_op | source)
XLA Modules:
  0.0 138.3 jit_solution(10076368631021912159)
XLA Ops:
  0.6 135.4 %shard_map.205 = (bf16[528,256]{1,0:T(8,128)(2,1)}, bf16[2,6,32,896]{3,2,1,0:T(8,128)(2,1)}) custom-call(bf16[512,256]{1,0:T(8,128)(2,1)} %x_ref.1, bf16[512,256]{1,0:T(8,128)(2,1)} %dy_ref.1, bf16[256,256]{1,0:T(8,128)(2,1)} %dense1.1, bf16[256,256]{1,0:T(8,128)(2,1)} %dense2.1, s32[2,512]{1,0:T(2,128)} %bitcast.6, f32[2,512]{1,0:T(2,128)} %bitcast.7, ...), custom_call_target="tpu_custom_call" | custom-call | tf_op jit(solution)/shard_map/pallas_call | solution.py:644
  136.0 2.1 %shard_map.206 = (bf16[512,256]{1,0:T(8,128)(2,1)}, bf16[8,256]{1,0:T(8,128)(2,1)}, bf16[2,32,896]{2,1,0:T(8,128)(2,1)}, bf16[2,32,896]{2,1,0:T(8,128)(2,1)}, bf...) custom-call(bf16[528,256]{1,0:T(8,128)(2,1)} %get-tuple-element.20.t, ...), custom_call_target="tpu_custom_call" | custom-call | tf_op jit(solution)/shard_map/pallas_call | solution.py:671
